TPU v7x, 32 devices: a whole 2x2x4 slice. The times are simulated.
32 devices in a mesh: groups: 2 (over x), blk: 4 (over y, core), col: 4 (over z).
Axes of the slice: x: 2, y: 2, z: 4, core: 2. Of those that a mesh axis runs over, the one named last changes fastest.
Arguments:
- pair_block: bfloat16 [4096, 16384], P(('groups', 'blk'), 'col'), parts along dimension 0, may hold values from -1.5 to 1.5
- occ_energy: float32 [2], P('groups'), parts along dimension 0, may hold values from -1.5 to -0.3
- virt_energy: float32 [4096], P('groups'), parts along dimension 0, may hold values from 0.2 to 3
- frequency: float32 [2], P('groups'), parts along dimension 0, may hold values from 0.2 to 2
Outputs:
- dielectric: float32 [32768, 16384], P(('groups', 'col'), 'blk'), parts along dimension 0
There are 2 independent parts, one for each index of `groups`. A program takes and returns all parts, laid end to end along the dimension named above; each array names one. Nothing has to cross between parts.
All inputs are finite; a program needn't handle non-finite values.
Results may differ from a plain program's by a relative error of at most 0.0027.
Values may be sent and summed in bfloat16 or wider, within the bound.
No kernel may reach another device: no remote copies, remote signals or barrier semaphores. Data moves between devices by JAX's collectives and lax.ppermute only.
A program may use at most 192 MiB of HBM per device.

v0:
```python
import jax
import jax.numpy as jnp
from jax import lax
from jax.sharding import PartitionSpec as P


def pair_weights(occ_energy, virt_energy, frequency):
    gap = (virt_energy[None, :] - occ_energy[:, None]).reshape(-1)
    return 2.0 * gap / (gap * gap + frequency[0] * frequency[0])


def shards(pair_block, occ_energy, virt_energy, frequency):
    weights = pair_weights(occ_energy, virt_energy, frequency)
    row_full = lax.all_gather(pair_block, "col", axis=1, tiled=True)
    column_slab = lax.all_to_all(row_full, "blk", split_axis=1, concat_axis=0, tiled=True)
    scaled = (
        lax.all_gather(pair_block, "blk", axis=0, tiled=True).astype(jnp.float32) * weights[:, None]
    ).astype(jnp.bfloat16)
    return lax.dot_general(
        scaled, column_slab, (((0,), (0,)), ((), ())), preferred_element_type=jnp.float32
    )


def solution(mesh):
    return jax.shard_map(
        shards,
        mesh=mesh,
        in_specs=(P(("groups", "blk"), "col"), P("groups"), P("groups"), P("groups")),
        out_specs=P(("groups", "col"), "blk"),
        check_vma=False,
    )
```

profile of v0, /device:TPU:0, one launch (start us, length us, event | category | flops | bytes accessed | tf_op | source)
XLA Modules:
  0.0 691.5 jit_solution(8358652491445676149)
XLA Ops:
  6.5 0.0 all-gather.5.cloned.1.call-start
  6.5 6.4 copy.5
  12.9 0.0 all-gather.5.cloned.1.call-update
  13.0 0.0 all-gather.3.cloned.1.call-start
  13.0 0.7 all-gather.3.cloned.1.call-update
  13.7 288.9 %all-gather.5.cloned.1.call-done = bf16[512,16384]{0,1:T(8,128)(2,1)} async-done(((bf16[512,4096]{0,1:T(8,128)(2,1)}), bf16[512,16384]{0,1:T(8,128)(2,1)}) %all-gather.5.cloned.1.call-update) | async-done | bytes 16777232 | tf_op jit(solution)/shard_map/all_gather | solution.py:14
  302.6 0.0 copy-start
  302.6 7.3 %all-to-all-start = ((bf16[512,4,4096]{0,2,1:T(8,128)(2,1)}), bf16[512,4,4096]{0,2,1:T(8,128)(2,1)}, u32[]{:S(2)}, u32[]{:S(2)}) async-start(bf16[512,4,4096]{0,2,1:T(8,128)(2,1)} %bitcast.8), calls=%async_computation | async-start | bytes 33554432 | tf_op jit(solution)/shard_map/all_to_all | solution.py:15
  311.2 0.0 copy-done
  311.2 271.6 %all-to-all-done = bf16[512,4,4096]{0,2,1:T(8,128)(2,1)} async-done(((bf16[512,4,4096]{0,2,1:T(8,128)(2,1)}), bf16[512,4,4096]{0,2,1:T(8,128)(2,1)}, u32[]{:S(2)}, u32[]{:S(2)}) %all-to-all-start) | async-done | bytes 16777248 | tf_op jit(solution)/shard_map/all_to_all | solution.py:15
  582.8 20.7 %copy.6 = bf16[4,512,4096]{2,1,0:T(8,128)(2,1)} copy(bf16[4,512,4096]{1,2,0:T(8,128)(2,1)} %bitcast.3) | data formatting | bytes 33554432 | tf_op jit(solution)/shard_map/all_to_all | solution.py:15
  603.5 0.0 all-gather.3.cloned.1.call-done
  603.5 81.2 %fusion = f32[4096,4096]{1,0:T(8,128)} fusion(bf16[2048,4096]{1,0:T(8,128)(2,1)} %bitcast.9, bf16[2048,4096]{1,0:T(8,128)(2,1)} %all-gather.3.cloned.1.call-done, f32[2048]{0:T(1024)S(1)} %add_divide_fusion), kind=kOutput, calls=%fused_computation.1 | convolution fusion | flops 68744642560 | bytes 100671488 | tf_op jit(solution)/shard_map/dot_general | solution.py:19
  (1 shorter events, 0.0 us)
Async XLA Ops:
  6.5 296.1 %all-gather.5.cloned.1.call-start = ((), (), s32[]{:S(2)}) async-start(), calls=%async_computation.2 | async-start | bytes 20971520 | tf_op jit(solution)/shard_map/all_gather | solution.py:14
  13.0 590.5 %all-gather.3.cloned.1.call-start = ((), (), s32[]{:S(2)}) async-start(), calls=%async_computation.1 | async-start | bytes 20971520 | tf_op jit(solution)/shard_map/all_gather | solution.py:17
  302.6 8.6 %copy-start = (f32[2048]{0:T(1024)S(1)}, f32[2048]{0:T(1024)}, u32[]{:S(2)}) copy-start(f32[2048]{0:T(1024)} %param.6) | copy-start | bytes 24580
  302.6 280.2 %all-to-all-start = ((bf16[512,4,4096]{0,2,1:T(8,128)(2,1)}), bf16[512,4,4096]{0,2,1:T(8,128)(2,1)}, u32[]{:S(2)}, u32[]{:S(2)}) async-start(bf16[512,4,4096]{0,2,1:T(8,128)(2,1)} %bitcast.8), calls=%async_computation | async-start | bytes 33554432 | tf_op jit(solution)/shard_map/all_to_all | solution.py:15
Sparse Core Ops, SparseCore 0:
  13.1 289.4 all-gather.4
  304.2 194.0 all-gather.2
where the time goes:
time: 692 us; the launch traced here: 691 us
  waiting for transfers between devices  561 us (81%)
  matrix products  81.2 us (12%)
  local copies, waits for them, and re-layouts  27.1 us (4%)
  between operations  14.7 us (2%)
  starting transfers between devices  7.3 us (1%)
    all_gather x1, waiting for transfers between devices, shards(): row_full = lax.all_gather(pair_block, 'col', axis=1, tiled=True)  289 us
    all_to_all x1, waiting for transfers between devices, shards(): lax.all_to_all(row_full, 'blk', split_axis=1, concat_axis=0, tiled=True)  272 us
    dot_general x1, matrix products, shards(): lax.dot_general(scaled, column_slab, (((0,), (0,)), ((), ())), preferred_...  81.2 us
    all_to_all x1, local copies, waits for them, and re-layouts, shards(): lax.all_to_all(row_full, 'blk', split_axis=1, concat_axis=0, tiled=True)  20.7 us
  transfers between devices with their start and end apart: 3, of which 2 were waited for; matrix products, arithmetic and copies ran while one was open for 3% of the time, Pallas kernels for 0%

commit v1 on v0

--- a/solution.py
+++ b/solution.py
@@ -1,7 +1,17 @@
+import functools
 import jax
 import jax.numpy as jnp
 from jax import lax
 from jax.sharding import PartitionSpec as P
+
+
+def finish_digits(sample, k_dim):
+    m_next = lax.all_gather(sample, "col")
+    d_next = jnp.concatenate(m_next, axis=k_dim)
+    return d_next
+
+
+axis_part_launch = functools.partial(finish_digits, k_dim=1)
 
 
 def pair_weights(occ_energy, virt_energy, frequency):
@@ -11,7 +21,7 @@
 
 def shards(pair_block, occ_energy, virt_energy, frequency):
     weights = pair_weights(occ_energy, virt_energy, frequency)
-    row_full = lax.all_gather(pair_block, "col", axis=1, tiled=True)
+    row_full = axis_part_launch(pair_block)
     column_slab = lax.all_to_all(row_full, "blk", split_axis=1, concat_axis=0, tiled=True)
     scaled = (
         lax.all_gather(pair_block, "blk", axis=0, tiled=True).astype(jnp.float32) * weights[:, None]

time: 692 us -> 667 us (0.964)
  local copies, waits for them, and re-layouts: 27.1 us -> 0.01 us
    all_to_all x1, waiting for transfers between devices: 272 us -> 84.5 us  [shards(): lax.all_to_all(row_full, 'blk', split_axis=1, concat_axis=0, tiled=True)]
    all_gather x1, waiting for transfers between devices: 0.01 us -> 187 us  [shards(): lax.all_gather(pair_block, 'blk', axis=0, tiled=True).astype(jnp.float32)]
    all_to_all x1 -> x0, local copies, waits for them, and re-layouts: 20.7 us -> none  [shards(): lax.all_to_all(row_full, 'blk', split_axis=1, concat_axis=0, tiled=True)]
  transfers between devices with their start and end apart: 3 -> 3, of which waited for: 2 -> 3; matrix products, arithmetic and copies ran while one was open for 3% -> 0% of each run, Pallas kernels for 0% -> 0%
where the time goes in v1:
time: 667 us
  waiting for transfers between devices  563 us (84%)
  matrix products  81.1 us (12%)
  between operations  14.7 us (2%)
  starting transfers between devices  7.3 us (1%)
    all_gather x1, waiting for transfers between devices, finish_digits(): m_next = lax.all_gather(sample, 'col')  290 us
    all_gather x1, waiting for transfers between devices, shards(): lax.all_gather(pair_block, 'blk', axis=0, tiled=True).astype(jnp.float32)  187 us
    all_to_all x1, waiting for transfers between devices, shards(): lax.all_to_all(row_full, 'blk', split_axis=1, concat_axis=0, tiled=True)  84.5 us
    dot_general x1, matrix products, shards(): lax.dot_general(scaled, column_slab, (((0,), (0,)), ((), ())), preferred_...  81.1 us
  transfers between devices with their start and end apart: 3, of which 3 were waited for; matrix products, arithmetic and copies ran while one was open for 0% of the time, Pallas kernels for 0%

profile of v1, /device:TPU:0, one launch (start us, length us, event | category | flops | bytes accessed | tf_op | source)
XLA Modules:
  0.0 666.6 jit_solution(17955778352746648957)
XLA Ops:
  6.5 0.0 all-gather.6.cloned.1.call-start
  6.5 0.7 all-gather.6.cloned.1.call-update
  7.3 0.0 all-gather.4.cloned.1.call-start
  7.3 0.7 all-gather.4.cloned.1.call-update
  8.0 290.4 %all-gather.6.cloned.1.call-done = bf16[2048,4096]{1,0:T(8,128)(2,1)} async-done(((bf16[512,4096]{1,0:T(8,128)(2,1)}), bf16[2048,4096]{1,0:T(8,128)(2,1)}) %all-gather.6.cloned.1.call-update) | async-done | bytes 16777232 | tf_op jit(solution)/shard_map/all_gather | solution.py:9
  298.4 0.0 copy-start
  298.4 7.3 %all-to-all-start = ((bf16[512,4,4096]{2,0,1:T(8,128)(2,1)}), bf16[512,4,4096]{2,0,1:T(8,128)(2,1)}, u32[]{:S(2)}, u32[]{:S(2)}) async-start(bf16[512,4,4096]{2,0,1:T(8,128)(2,1)} %bitcast.11), calls=%async_computation | async-start | bytes 33554432 | tf_op jit(solution)/shard_map/all_to_all | solution.py:25
  307.0 0.0 copy-done
  307.0 187.1 %all-gather.4.cloned.1.call-done = bf16[2048,4096]{1,0:T(8,128)(2,1)} async-done(((bf16[512,4096]{1,0:T(8,128)(2,1)}), bf16[2048,4096]{1,0:T(8,128)(2,1)}) %all-gather.4.cloned.1.call-update) | async-done | bytes 16777232 | tf_op jit(solution)/shard_map/all_gather | solution.py:27
  494.1 84.5 %all-to-all-done = bf16[512,4,4096]{2,0,1:T(8,128)(2,1)} async-done(((bf16[512,4,4096]{2,0,1:T(8,128)(2,1)}), bf16[512,4,4096]{2,0,1:T(8,128)(2,1)}, u32[]{:S(2)}, u32[]{:S(2)}) %all-to-all-start) | async-done | bytes 16777248 | tf_op jit(solution)/shard_map/all_to_all | solution.py:25
  578.6 81.1 %fusion = f32[4096,4096]{1,0:T(8,128)} fusion(bf16[2048,4096]{1,0:T(8,128)(2,1)} %bitcast.5, bf16[2048,4096]{1,0:T(8,128)(2,1)} %all-gather.4.cloned.1.call-done, f32[2048]{0:T(1024)S(1)} %add_divide_fusion), kind=kOutput, calls=%fused_computation.1 | convolution fusion | flops 68744642560 | bytes 100671488 | tf_op jit(solution)/shard_map/dot_general | solution.py:29
  (1 shorter events, 0.0 us)
Async XLA Ops:
  6.5 291.9 %all-gather.6.cloned.1.call-start = ((), (), s32[]{:S(2)}) async-start(), calls=%async_computation.2 | async-start | bytes 20971520 | tf_op jit(solution)/shard_map/all_gather | solution.py:9
  7.3 486.8 %all-gather.4.cloned.1.call-start = ((), (), s32[]{:S(2)}) async-start(), calls=%async_computation.1 | async-start | bytes 20971520 | tf_op jit(solution)/shard_map/all_gather | solution.py:27
  298.4 8.6 %copy-start = (f32[2048]{0:T(1024)S(1)}, f32[2048]{0:T(1024)}, u32[]{:S(2)}) copy-start(f32[2048]{0:T(1024)} %param.6) | copy-start | bytes 24580
  298.4 280.2 %all-to-all-start = ((bf16[512,4,4096]{2,0,1:T(8,128)(2,1)}), bf16[512,4,4096]{2,0,1:T(8,128)(2,1)}, u32[]{:S(2)}, u32[]{:S(2)}) async-start(bf16[512,4,4096]{2,0,1:T(8,128)(2,1)} %bitcast.11), calls=%async_computation | async-start | bytes 33554432 | tf_op jit(solution)/shard_map/all_to_all | solution.py:25
Sparse Core Ops, SparseCore 0:
  8.9 289.4 all-gather.5
  300.0 194.0 all-gather.3

commit v2 on v0

--- a/solution.py
+++ b/solution.py
@@ -2,6 +2,19 @@
 import jax.numpy as jnp
 from jax import lax
 from jax.sharding import PartitionSpec as P
+
+
+def apply_samples_all_on_mesh(inp, across):
+    clean = jnp.concatenate(
+        lax.all_to_all(
+            jnp.stack(jnp.split(inp, lax.axis_size(across), axis=1)),
+            across,
+            split_axis=0,
+            concat_axis=0,
+        ),
+        axis=0,
+    )
+    return clean
 
 
 def pair_weights(occ_energy, virt_energy, frequency):
@@ -12,7 +25,7 @@
 def shards(pair_block, occ_energy, virt_energy, frequency):
     weights = pair_weights(occ_energy, virt_energy, frequency)
     row_full = lax.all_gather(pair_block, "col", axis=1, tiled=True)
-    column_slab = lax.all_to_all(row_full, "blk", split_axis=1, concat_axis=0, tiled=True)
+    column_slab = apply_samples_all_on_mesh(row_full, "blk")
     scaled = (
         lax.all_gather(pair_block, "blk", axis=0, tiled=True).astype(jnp.float32) * weights[:, None]
     ).astype(jnp.bfloat16)

time: 692 us -> 670 us (0.968)
  local copies, waits for them, and re-layouts: 27.1 us -> 6.61 us
  waiting for transfers between devices: 561 us -> 551 us
  other arithmetic: 0.01 us -> 8.76 us
    all_to_all x1, waiting for transfers between devices: 272 us -> 100 us  [apply_samples_all_on_mesh(): lax.all_to_all(jnp.stack(jnp.split(inp, lax.axis_size(across), axis=1)),...]
    all_gather x1, waiting for transfers between devices: 0.01 us -> 159 us  [shards(): lax.all_gather(pair_block, 'blk', axis=0, tiled=True).astype(jnp.float32)]
    all_to_all x1 -> x0, local copies, waits for them, and re-layouts: 20.7 us -> none  [shards(): lax.all_to_all(row_full, 'blk', split_axis=1, concat_axis=0, tiled=True)]
    another operation x0 -> x1, other arithmetic: none -> 8.75 us  [apply_samples_all_on_mesh(): jnp.stack(jnp.split(inp, lax.axis_size(across), axis=1))]
  transfers between devices with their start and end apart: 3 -> 3, of which waited for: 2 -> 3; matrix products, arithmetic and copies ran while one was open for 3% -> 2% of each run, Pallas kernels for 0% -> 0%
where the time goes in v2:
time: 670 us
  waiting for transfers between devices  551 us (82%)
  matrix products  81.2 us (12%)
  between operations  14.7 us (2%)
  other arithmetic  8.76 us (1%)
  starting transfers between devices  7.48 us (1%)
    all_gather x1, waiting for transfers between devices, shards(): row_full = lax.all_gather(pair_block, 'col', axis=1, tiled=True)  290 us
    all_gather x1, waiting for transfers between devices, shards(): lax.all_gather(pair_block, 'blk', axis=0, tiled=True).astype(jnp.float32)  159 us
    all_to_all x1, waiting for transfers between devices, apply_samples_all_on_mesh(): lax.all_to_all(jnp.stack(jnp.split(inp, lax.axis_size(across), axis=1)),...  100 us
    dot_general x1, matrix products, shards(): lax.dot_general(scaled, column_slab, (((0,), (0,)), ((), ())), preferred_...  81.2 us
  transfers between devices with their start and end apart: 3, of which 3 were waited for; matrix products, arithmetic and copies ran while one was open for 2% of the time, Pallas kernels for 0%

profile of v2, /device:TPU:0, one launch (start us, length us, event | category | flops | bytes accessed | tf_op | source)
XLA Modules:
  0.0 669.8 jit_solution(16342548784936701926)
XLA Ops:
  6.5 0.0 all-gather.5.cloned.1.call-start
  6.5 0.7 all-gather.5.cloned.1.call-update
  7.3 0.0 all-gather.3.cloned.1.call-start
  7.3 0.7 all-gather.3.cloned.1.call-update
  8.0 290.4 %all-gather.5.cloned.1.call-done = bf16[512,16384]{1,0:T(8,128)(2,1)} async-done(((bf16[512,4096]{1,0:T(8,128)(2,1)}), bf16[512,16384]{1,0:T(8,128)(2,1)}) %all-gather.5.cloned.1.call-update) | async-done | bytes 16777232 | tf_op jit(solution)/shard_map/all_gather | solution.py:27
  298.4 6.6 slice_bitcast_fusion.3
  305.0 8.7 %pad_maximum_fusion = bf16[4,512,4096]{2,1,0:T(8,128)(2,1)} fusion(bf16[1,512,4096]{2,1,0:T(8,128)(2,1)S(1)} %get-tuple-element.6, bf16[1,512,4096]{2,1,0:T(8,128)(2,1)S(1)} %get-tuple-element.7, bf16[1,512,4096]{2,1,0:T(8,128)(2,1)S(1)} %get-tuple-element.8, bf16[1,512,4096]{2,1,0:T(8,128)(2,1)S(1)} %get-tuple-element.5), kind=kLoop, calls=%fused_computation.2 | loop fusion | flops 25165824 | bytes 33554432 | tf_op jit(solution)/shard_map/stack | solution.py:10
  313.8 0.0 copy-start
  313.8 7.4 %all-to-all-start = ((bf16[4,512,4096]{2,1,0:T(8,128)(2,1)}), bf16[4,512,4096]{2,1,0:T(8,128)(2,1)}, u32[]{:S(2)}, u32[]{:S(2)}) async-start(bf16[4,512,4096]{2,1,0:T(8,128)(2,1)} %pad_maximum_fusion), calls=%async_computation | async-start | bytes 33554432 | tf_op jit(solution)/shard_map/all_to_all | solution.py:9
  322.5 0.0 copy-done
  322.5 159.1 %all-gather.3.cloned.1.call-done = bf16[2048,4096]{1,0:T(8,128)(2,1)} async-done(((bf16[512,4096]{1,0:T(8,128)(2,1)}), bf16[2048,4096]{1,0:T(8,128)(2,1)}) %all-gather.3.cloned.1.call-update) | async-done | bytes 16777232 | tf_op jit(solution)/shard_map/all_gather | solution.py:30
  481.7 100.1 %all-to-all-done = bf16[4,512,4096]{2,1,0:T(8,128)(2,1)} async-done(((bf16[4,512,4096]{2,1,0:T(8,128)(2,1)}), bf16[4,512,4096]{2,1,0:T(8,128)(2,1)}, u32[]{:S(2)}, u32[]{:S(2)}) %all-to-all-start) | async-done | bytes 16777248 | tf_op jit(solution)/shard_map/all_to_all | solution.py:9
  581.8 81.2 %fusion = f32[4096,4096]{1,0:T(8,128)} fusion(bf16[2048,4096]{1,0:T(8,128)(2,1)} %bitcast.6, bf16[2048,4096]{1,0:T(8,128)(2,1)} %all-gather.3.cloned.1.call-done, f32[2048]{0:T(1024)S(1)} %add_divide_fusion), kind=kOutput, calls=%fused_computation.1 | convolution fusion | flops 68744642560 | bytes 100671488 | tf_op jit(solution)/shard_map/dot_general | solution.py:32
  (1 shorter events, 0.0 us)
Async XLA Ops:
  6.5 291.9 %all-gather.5.cloned.1.call-start = ((), (), s32[]{:S(2)}) async-start(), calls=%async_computation.2 | async-start | bytes 20971520 | tf_op jit(solution)/shard_map/all_gather | solution.py:27
  7.3 474.4 %all-gather.3.cloned.1.call-start = ((), (), s32[]{:S(2)}) async-start(), calls=%async_computation.1 | async-start | bytes 20971520 | tf_op jit(solution)/shard_map/all_gather | solution.py:30
  313.8 8.7 %copy-start = (f32[2048]{0:T(1024)S(1)}, f32[2048]{0:T(1024)}, u32[]{:S(2)}) copy-start(f32[2048]{0:T(1024)} %param.6) | copy-start | bytes 24580
  313.8 268.0 %all-to-all-start = ((bf16[4,512,4096]{2,1,0:T(8,128)(2,1)}), bf16[4,512,4096]{2,1,0:T(8,128)(2,1)}, u32[]{:S(2)}, u32[]{:S(2)}) async-start(bf16[4,512,4096]{2,1,0:T(8,128)(2,1)} %pad_maximum_fusion), calls=%async_computation | async-start | bytes 33554432 | tf_op jit(solution)/shard_map/all_to_all | solution.py:9
Sparse Core Ops, SparseCore 0:
  8.9 289.4 all-gather.4
  300.0 181.6 all-gather.2
